TPU v7x, 256 devices: a whole 4x4x8 slice. The times are simulated.
256 devices in a mesh: grp: 2 (over x_hi), seq: 64 (over z, y, core), mp: 2 (over x_lo).
Axes of the slice: x: 4 (x_hi: 2, x_lo: 2; x = x_hi * 2 + x_lo), y: 4, z: 8, core: 2. Of those that a mesh axis runs over, the one named last changes fastest.
Arguments:
- frames: bfloat16 [12288, 8192], P(('grp', 'seq'), 'mp'), may hold values from -80 to 80
- token_session: int32 [12288], P(('grp', 'seq')), may hold values from 0 to 1023, as said below
- ln_gain: float32 [8192], P('mp'), may hold values from 0.3 to 1.7
- w_key: bfloat16 [8192, 512], P('mp'), may hold values from -0.0625 to 0.0625
- w_value: bfloat16 [8192, 512], P('mp'), may hold values from -0.0625 to 0.0625
- k_bias: float32 [512], P('mp'), may hold values from -4 to 4
- v_bias: float32 [512], P('mp'), may hold values from -4 to 4
- queries: bfloat16 [1024, 4096], P(('grp', 'seq'), 'mp'), may hold values from -4 to 4
- cache_key: bfloat16 [1024, 128, 512], P(('grp', 'seq'), None, 'mp'), may hold values from -11 to 11
- cache_value: bfloat16 [1024, 128, 512], P(('grp', 'seq'), None, 'mp'), may hold values from -6 to 6
- cache_start: int32 [1024], P(('grp', 'seq')), may hold values from 0 to 127
- cache_len: int32 [1024], P(('grp', 'seq')), may hold values from 1 to 128
Outputs:
- attended: bfloat16 [1024, 4096], P(('grp', 'seq'), 'mp')
Inputs may be any that keep to these rules, and one draw needn't show every extreme that they name: `token_session`: each new frame token names a session; within the rows of one device at most 2 rows name sessions of one block of 8 consecutive sessions, and in every draw one such block gets exactly 2 rows from every device.
All inputs are finite; a program needn't handle non-finite values.
Results may differ from a plain program's by a relative error of at most 0.0023.
The roundings to bfloat16 on the way count: a program that leaves them out, or rounds other values in their place, can miss the bound.
Values may be sent and summed in bfloat16 or wider, within the bound.
A program may use at most 64 MiB of HBM per device.

v0:
```python
import jax
import jax.numpy as jnp
from jax import lax
from jax.sharding import PartitionSpec as P

D = 8192
HEAD = 128
GROUP = 8


epsilon = 1e-06


def total_of_pieces(shard, axis):
    blocks = lax.all_gather(shard, axis)
    return blocks.sum(axis=0)


def split_up(shard, dim, length):
    shape = shard.shape
    blocks = shard.reshape(*shape[:dim], length, shape[dim] // length, *shape[dim + 1 :])
    return jnp.moveaxis(blocks, dim, 0)


def sum_at_owner(shard, axis, dim):
    length = lax.axis_size(axis)
    blocks = lax.all_to_all(split_up(shard, dim, length), axis, 0, 0, tiled=True)
    return jnp.sum(blocks, axis=0)


def side_by_side(arrays, axis, dim, along):
    ends, at = ([], 0)
    for a in arrays[:-1]:
        at += a.shape[along]
        ends.append(at)
    both = jnp.concatenate(arrays, axis=along)
    return tuple(jnp.split(sum_at_owner(both, axis, dim), ends, axis=along))


def in_one_piece(arrays, axis, split_dim, concat_dim, along):
    ends, at = ([], 0)
    for a in arrays[:-1]:
        at += a.shape[along]
        ends.append(at)
    both = jnp.concatenate(arrays, axis=along)
    return tuple(
        jnp.split(
            lax.all_to_all(both, axis, split_axis=split_dim, concat_axis=concat_dim, tiled=True),
            ends,
            axis=along,
        )
    )


def project(frame_rows, ln_gain, w_key, w_value, k_bias, v_bias):
    values32 = frame_rows.astype(jnp.float32)
    partial_squares = jnp.sum(values32 * values32, axis=1)
    squares = total_of_pieces(partial_squares, "mp")
    inverse_rms = lax.rsqrt(squares / D + epsilon)
    normed = (values32 * inverse_rms[:, None] * ln_gain[None, :]).astype(jnp.bfloat16)
    part_key = jnp.dot(normed, w_key, preferred_element_type=jnp.float32)
    part_value = jnp.dot(normed, w_value, preferred_element_type=jnp.float32)
    key_sums, value_sums = side_by_side((part_key, part_value), "mp", 1, 0)
    new_keys = (key_sums + k_bias[None, :]).astype(jnp.bfloat16)
    new_values = (value_sums + v_bias[None, :]).astype(jnp.bfloat16)
    return (new_keys, new_values)


def slot_sources(token_session, per_shard, partition_count, capacity):
    row_count = token_session.shape[0]
    target = token_session // per_shard
    one_hot = (target[:, None] == jnp.arange(partition_count, dtype=jnp.int32)[None, :]).astype(
        jnp.int32
    )
    order_in = jnp.sum((jnp.cumsum(one_hot, axis=0) - one_hot) * one_hot, axis=1)
    slot_index = target * capacity + order_in
    matches = (
        slot_index[None, :] == jnp.arange(partition_count * capacity, dtype=jnp.int32)[:, None]
    )
    source = jnp.sum(jnp.where(matches, jnp.arange(row_count, dtype=jnp.int32)[None, :], 0), axis=1)
    filled = jnp.any(matches, axis=1)
    sessions = jnp.where(filled, jnp.mod(token_session[source], per_shard), -1)
    return (source, filled, sessions)


def local(
    frames,
    token_session,
    ln_gain,
    w_key,
    w_value,
    k_bias,
    v_bias,
    queries,
    cache_key,
    cache_value,
    cache_start,
    cache_len,
):
    partition_count = lax.axis_size(("grp", "seq"))
    per_shard = queries.shape[0]
    rows_here = frames.shape[0]
    capacity = max(2, 5 * rows_here // (2 * partition_count) + 1)
    source, filled, sessions = slot_sources(token_session, per_shard, partition_count, capacity)
    session_slots = sessions.reshape(partition_count, capacity)
    nothing = jnp.zeros((), jnp.bfloat16)
    own_keys, own_values = project(frames, ln_gain, w_key, w_value, k_bias, v_bias)
    send_keys = jnp.where(filled[:, None], own_keys[source], nothing).reshape(
        partition_count, capacity, -1
    )
    send_values = jnp.where(filled[:, None], own_values[source], nothing).reshape(
        partition_count, capacity, -1
    )
    got_keys, got_values, got_sessions = (
        *in_one_piece((send_keys, send_values), ("grp", "seq"), 0, 0, 1),
        lax.all_to_all(session_slots, ("grp", "seq"), split_axis=0, concat_axis=0, tiled=True),
    )
    new_keys = got_keys.reshape(partition_count * capacity, -1)
    new_values = got_values.reshape(partition_count * capacity, -1)
    new_sessions = got_sessions.reshape(-1)
    heads_kv = new_keys.shape[1] // HEAD
    window = cache_key.shape[1]
    score_scale = HEAD ** (-0.5)
    query_heads = queries.reshape(per_shard, heads_kv, GROUP, HEAD)
    cached_keys = cache_key.reshape(per_shard, window, heads_kv, HEAD)
    cached_values = cache_value.reshape(per_shard, window, heads_kv, HEAD)
    fresh_keys = new_keys.reshape(-1, heads_kv, HEAD)
    fresh_values = new_values.reshape(-1, heads_kv, HEAD)
    cached_scores = (
        jnp.einsum("sghd,swgd->sghw", query_heads, cached_keys, preferred_element_type=jnp.float32)
        * score_scale
    )
    positions = jnp.arange(window, dtype=jnp.int32)
    live_slots = jnp.mod(positions[None, :] - cache_start[:, None], window) < cache_len[:, None]
    cached_scores = jnp.where(live_slots[:, None, None, :], cached_scores, -jnp.inf)
    fresh_scores = (
        jnp.einsum("sghd,ngd->sghn", query_heads, fresh_keys, preferred_element_type=jnp.float32)
        * score_scale
    )
    own_rows = new_sessions[None, :] == jnp.arange(per_shard, dtype=jnp.int32)[:, None]
    fresh_scores = jnp.where(own_rows[:, None, None, :], fresh_scores, -jnp.inf)
    largest = jnp.maximum(jnp.max(cached_scores, axis=3), jnp.max(fresh_scores, axis=3))
    cached_exp = jnp.exp(cached_scores - largest[..., None])
    fresh_exp = jnp.exp(fresh_scores - largest[..., None])
    totals = jnp.sum(cached_exp, axis=3) + jnp.sum(fresh_exp, axis=3)
    cached_weights = (cached_exp / totals[..., None]).astype(jnp.bfloat16)
    fresh_weights = (fresh_exp / totals[..., None]).astype(jnp.bfloat16)
    attended = jnp.einsum(
        "sghw,swgd->sghd", cached_weights, cached_values, preferred_element_type=jnp.float32
    )
    attended = attended + jnp.einsum(
        "sghn,ngd->sghd", fresh_weights, fresh_values, preferred_element_type=jnp.float32
    )
    return attended.reshape(per_shard, -1).astype(jnp.bfloat16)


def solution(mesh):
    return jax.shard_map(
        local,
        mesh=mesh,
        in_specs=(
            P(("grp", "seq"), "mp"),
            P(("grp", "seq")),
            P("mp"),
            P("mp", None),
            P("mp", None),
            P("mp"),
            P("mp"),
            P(("grp", "seq"), "mp"),
            P(("grp", "seq"), None, "mp"),
            P(("grp", "seq"), None, "mp"),
            P(("grp", "seq")),
            P(("grp", "seq")),
        ),
        out_specs=P(("grp", "seq"), "mp"),
        check_vma=False,
    )
```

profile of v0, /device:TPU:1, one launch (start us, length us, event | category | flops | bytes accessed | tf_op | source)
XLA Modules:
  0.0 77.2 jit_solution(9004951143609793268)
XLA Ops:
  0.0 0.0 copy-start
  0.0 1.4 %fusion = f32[96]{0:T(128)S(1)} fusion(bf16[96,4096]{1,0:T(8,128)(2,1)} %param.12), kind=kLoop, calls=%fused_computation.5 | loop fusion | flops 1179552 | bytes 786816 | tf_op jit(solution)/shard_map/reduce_sum | solution.py:57
  1.5 1.3 %dynamic-slice = u32[1]{0:T(128)} dynamic-slice(u32[256]{0:T(256)} %constant.78, u32[]{:T(128)S(6)} %add.88), dynamic_slice_sizes={1} | dynamic-slice | bytes 12
  3.4 0.2 dynamic-update-slice
  3.6 4.3 %all-reduce = f32[192]{0:T(256)S(1)} all-reduce(f32[192]{0:T(256)S(1)} %dynamic-update-slice), channel_id=2, replica_groups=mesh['grp'=2,'seq'=64,'mp'=2] {'mp'}, use_global_device_ids=true, to_apply=%add | all-reduce | flops 192 | bytes 1536
  7.9 0.1 reshape.217
  8.1 0.0 copy-start.2
  8.1 0.0 copy-start.3
  8.1 0.0 copy-start.4
  8.1 3.4 %fusion.14 = f32[96,512]{1,0:T(8,128)S(1)} fusion(bf16[4096,512]{1,0:T(8,128)(2,1)} %param.16, bf16[96,4096]{1,0:T(8,128)(2,1)} %param.12, f32[4096]{0:T(1024)} %param.14, f32[96]{0:T(128)S(1)} %add_rsqrt_fusion), kind=kOutput, calls=%fused_computation.27 | convolution fusion | flops 404226048 | bytes 5194112 | tf_op jit(solution)/shard_map/dot_general | solution.py:62
  11.5 0.0 copy-done.2
  11.5 0.5 copy-done.3
  12.0 0.0 copy-done.4
  12.0 0.8 %fusion.16 = f32[96,512]{1,0:T(8,128)S(1)} fusion(bf16[4096,512]{1,0:T(8,128)(2,1)S(1)} %copy-done.3, bf16[96,4096]{1,0:T(8,128)(2,1)S(1)} %copy-done.2, f32[4096]{0:T(1024)S(1)} %copy-done.4, f32[96]{0:T(128)S(1)} %add_rsqrt_fusion), kind=kOutput, calls=%fused_computation.28 | convolution fusion | flops 404226048 | bytes 5194112 | tf_op jit(solution)/shard_map/dot_general | solution.py:61
  12.9 0.0 copy-start.1
  12.9 0.8 copy.118
  13.7 0.0 copy-start.6
  13.7 3.6 %all-to-all-start.1 = ((f32[2,192,256]{2,1,0:T(8,128)}), f32[2,192,256]{2,1,0:T(8,128)S(1)}, u32[]{:S(2)}, u32[]{:S(2)}) async-start(f32[2,192,256]{2,1,0:T(8,128)} %bitcast.50), calls=%async_computation.1 | async-start | bytes 786432 | tf_op jit(solution)/shard_map/all_to_all | solution.py:27
  17.3 0.0 copy-done.1
  17.3 0.1 fusion.29
  17.4 0.1 reduce_window_sum.11
  17.5 0.2 select_reduce_fusion.1
  17.7 0.1 select_reduce_fusion
  17.8 0.1 fusion.24
  17.9 0.2 broadcast_in_dim.88
  18.1 0.2 reduce_or.12
  18.3 1.9 %gather_fusion = s32[256]{0:T(256)S(1)} fusion(s32[96]{0:T(128)S(1)} %copy-done.1, s32[1024]{0:T(1024)S(1)} %pad_clamp_fusion), kind=kCustom, calls=%fused_computation | custom fusion | bytes 3072 | tf_op jit(solution)/shard_map/gather | solution.py:82
  20.2 0.1 gather.16
  20.3 0.7 fusion.26
  20.9 1.1 %all-to-all-done.1 = f32[2,192,256]{2,1,0:T(8,128)S(1)} async-done(((f32[2,192,256]{2,1,0:T(8,128)}), f32[2,192,256]{2,1,0:T(8,128)S(1)}, u32[]{:S(2)}, u32[]{:S(2)}) %all-to-all-start.1) | async-done | bytes 393248 | tf_op jit(solution)/shard_map/all_to_all | solution.py:27
  22.0 18.1 %all-to-all-start = ((s32[128,1,2]{2,1,0:T(1,128)}), s32[128,1,2]{2,1,0:T(1,128)S(1)}, u32[]{:S(2)}, u32[]{:S(2)}) async-start(s32[128,1,2]{2,1,0:T(1,128)} %bitcast.3), calls=%async_computation | async-start | bytes 131072 | tf_op jit(solution)/shard_map/all_to_all | solution.py:116
  40.2 0.0 copy-done.6
  40.2 0.0 copy-done.7
  40.2 1.2 %gather_fusion.1 = bf16[256,256]{1,0:T(8,128)(2,1)S(1)} fusion(bf16[96,256]{1,0:T(8,128)(2,1)S(1)} %get-tuple-element.7, s32[1024]{0:T(1024)S(1)} %pad_clamp_fusion), kind=kCustom, calls=%fused_computation.1 | custom fusion | bytes 263168 | tf_op jit(solution)/shard_map/gather | solution.py:108
  41.4 0.1 gather.18
  41.4 0.0 copy-start.8
  41.4 0.0 copy-start.9
  41.5 0.0 copy-start.5
  41.5 1.2 %gather_fusion.2 = bf16[256,256]{1,0:T(8,128)(2,1)S(1)} fusion(bf16[96,256]{1,0:T(8,128)(2,1)S(1)} %get-tuple-element.8, s32[1024]{0:T(1024)S(1)} %pad_clamp_fusion), kind=kCustom, calls=%fused_computation.2 | custom fusion | bytes 263168 | tf_op jit(solution)/shard_map/gather | solution.py:111
  42.6 0.1 gather.20
  42.7 0.3 broadcast_select_fusion.1
  43.0 1.0 %pad_maximum_fusion.1 = bf16[128,4,256]{2,1,0:T(4,128)(2,1)} fusion(bf16[128,2,256]{2,1,0:T(2,128)(2,1)S(1)} %get-tuple-element.10, bf16[128,2,256]{2,1,0:T(2,128)(2,1)S(1)} %get-tuple-element.9), kind=kLoop, calls=%fused_computation.24 | loop fusion | flops 524288 | bytes 524288 | tf_op jit(solution)/shard_map/concatenate | solution.py:45
  44.0 8.5 %all-to-all-done = s32[128,1,2]{2,1,0:T(1,128)S(1)} async-done(((s32[128,1,2]{2,1,0:T(1,128)}), s32[128,1,2]{2,1,0:T(1,128)S(1)}, u32[]{:S(2)}, u32[]{:S(2)}) %all-to-all-start) | async-done | bytes 1056 | tf_op jit(solution)/shard_map/all_to_all | solution.py:116
  52.5 5.8 %all-to-all-start.2 = ((bf16[128,4,256]{2,1,0:T(4,128)(2,1)}), bf16[128,4,256]{2,1,0:T(4,128)(2,1)S(1)}, u32[]{:S(2)}, u32[]{:S(2)}) async-start(bf16[128,4,256]{2,1,0:T(4,128)(2,1)} %pad_maximum_fusion.1), calls=%async_computation.2 | async-start | bytes 524288 | tf_op jit(solution)/shard_map/all_to_all | solution.py:48
  58.3 0.0 copy-done.8
  58.3 0.0 copy-done.9
  58.3 0.1 fusion.35
  58.4 0.0 copy-done
  58.4 0.0 copy-done.5
  58.4 0.5 fusion.41
  58.9 0.5 broadcast.177
  59.4 0.8 %reduce.3 = s32[128,2]{1,0:T(8,128)S(1)} reduce(s32[128,1,2]{2,1,0:T(1,128)S(1)} %all-to-all-done, s32[]{:T(128)} %broadcast.177), dimensions={1}, to_apply=%all_to_all.10.reduce_sub_computation.3 | reduce | bytes 2052 | tf_op jit(solution)/shard_map/all_to_all | solution.py:116
  60.2 0.1 eq.55
  60.4 14.6 %all-to-all-done.2 = bf16[128,4,256]{2,1,0:T(4,128)(2,1)S(1)} async-done(((bf16[128,4,256]{2,1,0:T(4,128)(2,1)}), bf16[128,4,256]{2,1,0:T(4,128)(2,1)S(1)}, u32[]{:S(2)}, u32[]{:S(2)}) %all-to-all-start.2) | async-done | bytes 262176 | tf_op jit(solution)/shard_map/all_to_all | solution.py:48
  75.0 0.2 fusion.39
  75.2 0.1 reshape_reshape.6
  75.3 0.3 fusion.40
  75.6 0.2 fusion.21
  75.8 0.2 fusion.28
  76.0 0.1 reshape_reshape.7
  76.1 0.0 copy-done.10
  76.1 0.3 fusion.9
  76.4 0.2 fusion.8
  76.6 0.6 copy.119
  (17 shorter events, 0.2 us)
Async XLA Ops:
  0.0 58.4 %copy-start = (bf16[8,128,256]{2,1,0:T(8,128)(2,1)S(1)}, bf16[8,128,256]{2,1,0:T(8,128)(2,1)}, u32[]{:S(2)}) copy-start(bf16[8,128,256]{2,1,0:T(8,128)(2,1)} %param.20) | copy-start | bytes 1572868
  8.1 3.5 %copy-start.2 = (bf16[96,4096]{1,0:T(8,128)(2,1)S(1)}, bf16[96,4096]{1,0:T(8,128)(2,1)}, u32[]{:S(2)}) copy-start(bf16[96,4096]{1,0:T(8,128)(2,1)} %param.12) | copy-start | bytes 2359300
  8.1 3.9 %copy-start.3 = (bf16[4096,512]{1,0:T(8,128)(2,1)S(1)}, bf16[4096,512]{1,0:T(8,128)(2,1)}, u32[]{:S(2)}) copy-start(bf16[4096,512]{1,0:T(8,128)(2,1)} %param.15) | copy-start | bytes 12582916
  8.1 3.9 %copy-start.4 = (f32[4096]{0:T(1024)S(1)}, f32[4096]{0:T(1024)}, u32[]{:S(2)}) copy-start(f32[4096]{0:T(1024)} %param.14) | copy-start | bytes 49156
  12.9 4.4 %copy-start.1 = (s32[96]{0:T(128)S(1)}, s32[96]{0:T(128)}, u32[]{:S(2)}) copy-start(s32[96]{0:T(128)} %param.13) | copy-start | bytes 1156
  13.7 26.5 %copy-start.6 = (f32[256]{0:T(256)S(1)}, f32[256]{0:T(256)}, u32[]{:S(2)}) copy-start(f32[256]{0:T(256)} %param.17) | copy-start | bytes 3076
  13.7 26.5 %copy-start.7 = (f32[256]{0:T(256)S(1)}, f32[256]{0:T(256)}, u32[]{:S(2)}) copy-start(f32[256]{0:T(256)} %param.18) | copy-start | bytes 3076
  13.7 8.3 %all-to-all-start.1 = ((f32[2,192,256]{2,1,0:T(8,128)}), f32[2,192,256]{2,1,0:T(8,128)S(1)}, u32[]{:S(2)}, u32[]{:S(2)}) async-start(f32[2,192,256]{2,1,0:T(8,128)} %bitcast.50), calls=%async_computation.1 | async-start | bytes 786432 | tf_op jit(solution)/shard_map/all_to_all | solution.py:27
  22.0 30.5 %all-to-all-start = ((s32[128,1,2]{2,1,0:T(1,128)}), s32[128,1,2]{2,1,0:T(1,128)S(1)}, u32[]{:S(2)}, u32[]{:S(2)}) async-start(s32[128,1,2]{2,1,0:T(1,128)} %bitcast.3), calls=%async_computation | async-start | bytes 131072 | tf_op jit(solution)/shard_map/all_to_all | solution.py:116
  41.4 16.9 %copy-start.8 = (s32[8]{0:T(128)S(1)}, s32[8]{0:T(128)}, u32[]{:S(2)}) copy-start(s32[8]{0:T(128)} %param.23) | copy-start | bytes 100
  41.4 16.9 %copy-start.9 = (s32[8]{0:T(128)S(1)}, s32[8]{0:T(128)}, u32[]{:S(2)}) copy-start(s32[8]{0:T(128)} %param.22) | copy-start | bytes 100
  41.5 17.0 %copy-start.5 = (bf16[8,2048]{1,0:T(8,128)(2,1)S(1)}, bf16[8,2048]{1,0:T(8,128)(2,1)}, u32[]{:S(2)}) copy-start(bf16[8,2048]{1,0:T(8,128)(2,1)} %param.19) | copy-start | bytes 98308
  44.0 32.1 %copy-start.10 = (bf16[8,128,256]{2,1,0:T(8,128)(2,1)S(1)}, bf16[8,128,256]{2,1,0:T(8,128)(2,1)}, u32[]{:S(2)}) copy-start(bf16[8,128,256]{2,1,0:T(8,128)(2,1)} %param.21) | copy-start | bytes 1572868
  52.5 22.6 %all-to-all-start.2 = ((bf16[128,4,256]{2,1,0:T(4,128)(2,1)}), bf16[128,4,256]{2,1,0:T(4,128)(2,1)S(1)}, u32[]{:S(2)}, u32[]{:S(2)}) async-start(bf16[128,4,256]{2,1,0:T(4,128)(2,1)} %pad_maximum_fusion.1), calls=%async_computation.2 | async-start | bytes 524288 | tf_op jit(solution)/shard_map/all_to_all | solution.py:48
where the time goes:
time: 77.6 us; the launch traced here: 77.2 us
  starting transfers between devices  27.5 us (35%)
  waiting for transfers between devices  24.2 us (31%)
  local copies, waits for them, and re-layouts  9.28 us (12%)
  matrix products  5.54 us (7%)
  other arithmetic  5.37 us (7%)
  blocking collectives  4.32 us (6%)
  between operations  1.01 us (1%)
    all_to_all x1, starting transfers between devices, local(): lax.all_to_all(session_slots, ('grp', 'seq'), split_axis=0, concat_axis=0...  18.1 us
    all_to_all x1, waiting for transfers between devices, in_one_piece(): lax.all_to_all(both, axis, split_axis=split_dim, concat_axis=concat_dim,...  14.6 us
    all_to_all x1, waiting for transfers between devices, local(): lax.all_to_all(session_slots, ('grp', 'seq'), split_axis=0, concat_axis=0...  8.48 us
    all_to_all x1, starting transfers between devices, in_one_piece(): lax.all_to_all(both, axis, split_axis=split_dim, concat_axis=concat_dim,...  5.84 us
    unnamed x1, blocking collectives  4.32 us
    all_to_all x1, starting transfers between devices, sum_at_owner(): lax.all_to_all(split_up(shard, dim, length), axis, 0, 0, tiled=True)  3.6 us
    dot_general x1, matrix products, project(): part_value = jnp.dot(normed, w_value, preferred_element_type=jnp.float32)  3.44 us
    unnamed x26, local copies, waits for them, and re-layouts  2.65 us
  transfers between devices with their start and end apart: 3, of which 3 were waited for; matrix products, arithmetic and copies ran while one was open for 12% of the time, Pallas kernels for 0%

commit v1 on v0

v1 whole, which is shorter than its diff:
```python
import functools

import jax
import jax.numpy as jnp
from jax import lax
from jax.experimental import pallas as pl
from jax.experimental.pallas import tpu as pltpu
from jax.sharding import PartitionSpec as P

HEAD = 128
GROUP = 8
EPSILON = 1e-6
MESH = pl.DeviceIdType.MESH

NZ, NY, NC, NG = 8, 4, 2, 2
PARTS = NG * NZ * NY * NC
F32 = jnp.float32
BF16 = jnp.bfloat16


def kernel(
    tok_hbm, frames_hbm, gain_hbm, wk_hbm, wv_hbm, kb_hbm, vb_hbm, q_hbm, ck_hbm, cv_hbm, start_hbm, len_hbm,
    out_ref,
    tok, frames, gain, weights, kb, vb, q, ck, cv, start, length,
    normed, square_out, square_in, part_out, part_in, own_part, onehot, send, recv, send_id, recv_id, cached,
    sem_in, sem_w, sem_sq, sem_part_s, sem_part_r, sem_data, sem_id, know1, know2, know3,
):
    g, s, m = lax.axis_index("grp"), lax.axis_index("seq"), lax.axis_index("mp")
    core, y, z = lax.rem(s, NC), lax.rem(s // NC, NY), s // (NC * NY)
    me = g * (NZ * NY * NC) + s
    rows, depth = frames.shape
    half = kb.shape[1]

    def seq_of(zz, yy, cc):
        return zz * (NY * NC) + yy * NC + cc

    def turned(dg, dz, dy, dc):
        return (
            lax.rem(g + dg, NG),
            seq_of(lax.rem(z + dz, NZ), lax.rem(y + dy, NY), lax.rem(core + dc, NC)),
            m,
        )

    other = (g, s, 1 - m)

    def tell(sem, devices):
        for device in devices:
            pl.semaphore_signal(sem, inc=1, device_id=device, device_id_type=MESH)

    barrier = pltpu.get_barrier_semaphore()
    far_core = seq_of(z, y, 1 - core)
    near = [
        other, (1 - g, s, 1 - m), (g, far_core, 1 - m), (1 - g, far_core, 1 - m), (g, far_core, m),
        turned(0, 1, 0, 0), turned(0, NZ - 1, 0, 0), turned(0, 0, 1, 0), turned(0, 0, NY - 1, 0),
    ]
    tell(barrier, near)

    chunk = 32
    loads = [
        pltpu.make_async_copy(
            frames_hbm.at[pl.ds(i * chunk, chunk)], frames.at[pl.ds(i * chunk, chunk)], sem_in.at[i]
        )
        for i in range(rows // chunk)
    ]
    n = len(loads)
    gain_load = pltpu.make_async_copy(gain_hbm, gain, sem_in.at[n])
    tok_load = pltpu.make_async_copy(tok_hbm, tok, sem_in.at[n + 1])
    small = [
        pltpu.make_async_copy(kb_hbm, kb, sem_in.at[n + 2]),
        pltpu.make_async_copy(vb_hbm, vb, sem_in.at[n + 3]),
    ]
    late = [
        pltpu.make_async_copy(q_hbm, q, sem_in.at[n + 4]),
        pltpu.make_async_copy(ck_hbm, ck, sem_in.at[n + 5]),
        pltpu.make_async_copy(cv_hbm, cv, sem_in.at[n + 6]),
        pltpu.make_async_copy(start_hbm, start, sem_in.at[n + 7]),
        pltpu.make_async_copy(len_hbm, length, sem_in.at[n + 8]),
    ]
    for load in loads:
        load.start()
    gain_load.start()
    tok_load.start()
    weight_loads = []
    for i, (source, side) in enumerate(((wk_hbm, 1 - m), (wv_hbm, 1 - m), (wk_hbm, m), (wv_hbm, m))):
        load = pltpu.make_async_copy(
            source.at[:, pl.ds(pl.multiple_of(side * half, half), half)], weights.at[i], sem_w.at[i]
        )
        load.start()
        weight_loads.append(load)
    for load in small + late:
        load.start()

    lanes = 128
    square_out[...] = jnp.zeros_like(square_out)
    sums = []
    for i, load in enumerate(loads):
        load.wait()
        total = jnp.zeros((chunk, lanes), F32)
        for j in range(depth // lanes):
            x = frames[pl.ds(i * chunk, chunk), pl.ds(j * lanes, lanes)].astype(F32)
            total = total + x * x
        sums.append(total)
    sums.append(jnp.zeros((lanes - rows, lanes), F32))
    own_squares = jnp.sum(jnp.concatenate(sums, axis=0).T, axis=0, keepdims=True)
    square_out[...] = own_squares
    pl.semaphore_wait(barrier, len(near))
    square_copy = pltpu.make_async_remote_copy(
        square_out, square_in, sem_sq.at[0], sem_sq.at[1], device_id=other, device_id_type=MESH
    )
    square_copy.start()
    tell(know1, [turned(0, 1, 0, 0), turned(0, NZ - 1, 0, 0), turned(0, 0, 1, 0), turned(0, 0, NY - 1, 0), other])

    tok_load.wait()
    row_at = lax.broadcasted_iota(jnp.int32, (1, lanes), 1)
    session = jnp.concatenate([tok[...].astype(F32), jnp.full((1, lanes - rows), -8.0 * PARTS, F32)], axis=1)
    block = jnp.floor(session * 0.125)
    within = session - block * 8.0
    block_here = jnp.broadcast_to(block, (lanes, lanes))
    lane_i = lax.broadcasted_iota(jnp.int32, (lanes, lanes), 1)
    sub_i = lax.broadcasted_iota(jnp.int32, (lanes, lanes), 0)
    before = (block_here.T == block_here) & (sub_i < lane_i)
    rank = jnp.sum(before.astype(F32), axis=0, keepdims=True)
    slot = jnp.where(row_at < rows, block * 2.0 + rank, -1.0)
    slot_here = jnp.broadcast_to(slot, (lanes, lanes))
    ids = []
    for j in range(2):
        hit = slot_here == (2 * sub_i + j).astype(F32)
        ids.append(jnp.sum(jnp.where(hit, within + 1.0, 0.0), axis=1, keepdims=True))
    id_here = jnp.where(lax.rem(lane_i // 4, 2) == 0, ids[0], ids[1])
    id_here = jnp.where(lane_i // 8 == lax.rem(me, 16), id_here, 0.0)
    send_id[...] = id_here.reshape(PARTS, 1, lanes)
    for p in range(8):
        big = lax.broadcasted_iota(jnp.int32, (lanes, lanes), 0)
        hit = jnp.broadcast_to(slot, (lanes, lanes)) == (big // 4 + p * 32).astype(F32)
        for c in range(4):
            onehot[pl.ds(p * lanes, lanes), pl.ds(c * lanes, lanes)] = jnp.where(
                hit & (lax.rem(big, 4) == c), 1.0, 0.0
            ).astype(BF16)

    pl.semaphore_wait(know1, 5)
    line = [turned(0, 0, d, 0) for d in range(1, NY)]
    tell(know2, [turned(0, 2, 0, 0), turned(0, NZ - 2, 0, 0)] + line)

    gain_load.wait()
    square_copy.wait()
    squares = square_out[...] + square_in[...]
    inverse = lax.rsqrt(squares / (2 * depth) + EPSILON)
    inverse = jnp.broadcast_to(inverse, (lanes, lanes)).T[:rows]
    for j in range(depth // lanes):
        cols = pl.ds(j * lanes, lanes)
        normed[:, cols] = (frames[:, cols].astype(F32) * inverse * gain[:, cols]).astype(BF16)

    pl.semaphore_wait(know2, 5)
    group = [
        turned(dg, 0, dy, dc) for dg in range(NG) for dy in range(NY) for dc in range(NC) if dg or dy or dc
    ]
    tell(know3, group)

    part_copies = []
    for i in range(4):
        weight_loads[i].wait()
        product = jnp.dot(normed[...], weights[i], preferred_element_type=F32)
        if i < 2:
            part_out[i] = product
            copy = pltpu.make_async_remote_copy(
                part_out.at[i], part_in.at[i], sem_part_s.at[i], sem_part_r.at[i], device_id=other, device_id_type=MESH
            )
            copy.start()
            part_copies.append(copy)
        else:
            own_part[i - 2] = product
    for load in small + late:
        load.wait()

    pl.semaphore_wait(know3, len(group))

    def peer(k):
        return turned(k // (NZ * NY * NC), lax.rem(k // (NY * NC), NZ), lax.rem(k // NC, NY), lax.rem(k, NC))

    @pl.loop(1, PARTS)
    def _(k):
        device = peer(k)
        to = device[0] * (NZ * NY * NC) + device[1]
        pltpu.make_async_remote_copy(
            send_id.at[to], recv_id.at[me], sem_id.at[0], sem_id.at[1], device_id=device, device_id_type=MESH
        ).start()

    recv_id[me] = send_id[me]

    heads = q.shape[1] // HEAD
    kv_heads = heads // GROUP
    per_shard = q.shape[0]
    stacked = jnp.concatenate([q[:, pl.ds(i * HEAD, HEAD)] for i in range(heads)], axis=0)
    scale = HEAD**-0.5
    window = ck.shape[1]
    slots = lax.broadcasted_iota(jnp.int32, (1, window), 1)
    row_session = lax.broadcasted_iota(jnp.int32, (GROUP * per_shard, lanes), 0)
    row_session = lax.rem(row_session, per_shard)
    for h in range(kv_heads):
        queries = stacked[h * GROUP * per_shard : (h + 1) * GROUP * per_shard]
        score = jnp.zeros((GROUP * per_shard, window), F32)
        for b in range(per_shard):
            keys = ck[b, :, pl.ds(h * HEAD, HEAD)]
            product = lax.dot_general(queries, keys, (((1,), (1,)), ((), ())), preferred_element_type=F32) * scale
            live = lax.rem(slots - start[b] + window, window) < length[b]
            product = jnp.where(live, product, -jnp.inf)
            score = jnp.where(row_session == b, product, score)
        cached[pl.ds(h * GROUP * per_shard, GROUP * per_shard)] = score

    parts = []
    for i, bias in enumerate((kb, vb)):
        part_copies[i].wait()
        whole = (own_part[i] + part_in[i] + bias[...]).astype(BF16)
        for h in range(kv_heads):
            parts.append(whole[:, h * HEAD : (h + 1) * HEAD])
            parts.append(jnp.zeros((lanes - rows, HEAD), BF16))
    table = jnp.concatenate(parts, axis=0)
    slotted = jnp.dot(onehot[...], table, preferred_element_type=F32).astype(BF16)
    send[...] = slotted.reshape(send.shape)

    @pl.loop(1, PARTS)
    def _(k):
        device = peer(k)
        to = device[0] * (NZ * NY * NC) + device[1]
        pltpu.make_async_remote_copy(
            send.at[to], recv.at[me], sem_data.at[0], sem_data.at[1], device_id=device, device_id_type=MESH
        ).start()

    recv[me] = send[me]

    everyone = pl.ds(0, PARTS - 1)
    pltpu.make_async_remote_copy(
        send_id.at[everyone], recv_id.at[everyone], sem_id.at[0], sem_id.at[1], device_id=other, device_id_type=MESH
    ).wait()
    lane_ids = [jnp.sum(recv_id[pl.ds(16 * i, 16)], axis=0) for i in range(8)]
    pltpu.make_async_remote_copy(
        send.at[everyone], recv.at[everyone], sem_data.at[0], sem_data.at[1], device_id=other, device_id_type=MESH
    ).wait()

    fresh_rows = recv[...].reshape(PARTS * 8, HEAD)
    fresh = lax.dot_general(stacked, fresh_rows, (((1,), (1,)), ((), ())), preferred_element_type=F32) * scale
    ids_row = jnp.concatenate(lane_ids, axis=1)
    shape = fresh.shape
    row_i = lax.broadcasted_iota(jnp.int32, shape, 0)
    col_i = lax.broadcasted_iota(jnp.int32, shape, 1)
    match = (ids_row == (lax.rem(row_i, per_shard) + 1).astype(F32)) & (
        lax.rem(col_i, 4) == row_i // (GROUP * per_shard)
    )
    fresh = jnp.where(match, fresh, -jnp.inf)
    held = cached[...]
    largest = jnp.maximum(jnp.max(held, axis=1, keepdims=True), jnp.max(fresh, axis=1, keepdims=True))
    held_exp = jnp.exp(held - largest)
    fresh_exp = jnp.exp(fresh - largest)
    total = jnp.sum(held_exp, axis=1, keepdims=True) + jnp.sum(fresh_exp, axis=1, keepdims=True)
    inverse_total = 1.0 / total
    held_weights = held_exp * inverse_total
    fresh_weights = pltpu.roll(fresh_exp * inverse_total, 2, 1).astype(BF16)
    result = jnp.dot(fresh_weights, fresh_rows, preferred_element_type=F32)
    for h in range(kv_heads):
        part = result[h * GROUP * per_shard : (h + 1) * GROUP * per_shard]
        mine = held_weights[h * GROUP * per_shard : (h + 1) * GROUP * per_shard]
        for b in range(per_shard):
            only = jnp.where(row_session == b, mine, 0.0).astype(BF16)
            part = part + jnp.dot(only, cv[b, :, pl.ds(h * HEAD, HEAD)], preferred_element_type=F32)
        for i in range(GROUP):
            out_ref[:, pl.ds((h * GROUP + i) * HEAD, HEAD)] = part[
                i * per_shard : (i + 1) * per_shard
            ].astype(BF16)


def local(
    frames, token_session, ln_gain, w_key, w_value, k_bias, v_bias, queries, cache_key, cache_value, cache_start,
    cache_len,
):
    rows, depth = frames.shape
    half = k_bias.shape[0]
    row = lambda a: a.reshape(1, -1)
    anywhere = pl.BlockSpec(memory_space=pltpu.HBM)
    dma = pltpu.SemaphoreType.DMA
    regular = pltpu.SemaphoreType.REGULAR
    vm = pltpu.VMEM
    return pl.pallas_call(
        kernel,
        out_shape=jax.ShapeDtypeStruct(queries.shape, BF16),
        in_specs=[anywhere] * 12,
        out_specs=pl.BlockSpec(memory_space=pltpu.VMEM),
        scratch_shapes=[
            vm((1, rows), jnp.int32), vm((rows, depth), BF16), vm((1, depth), F32), vm((4, depth, half), BF16),
            vm((1, half), F32), vm((1, half), F32), vm(queries.shape, BF16), vm(cache_key.shape, BF16),
            vm(cache_value.shape, BF16), pltpu.SMEM((8,), jnp.int32), pltpu.SMEM((8,), jnp.int32),
            vm((rows, depth), BF16), vm((1, 128), F32), vm((1, 128), F32), vm((2, rows, half), F32),
            vm((2, rows, half), F32), vm((2, rows, half), F32), vm((PARTS * 8, 512), BF16),
            vm((PARTS, 8, HEAD), BF16), vm((PARTS, 8, HEAD), BF16), vm((PARTS, 1, 128), F32), vm((PARTS, 1, 128), F32),
            vm((128, 128), F32),
            dma((16,)), dma((4,)), dma((2,)), dma((2,)), dma((2,)), dma((2,)), dma((2,)),
            regular, regular, regular,
        ],
        compiler_params=pltpu.CompilerParams(
            collective_id=0, has_side_effects=True, vmem_limit_bytes=67_000_000
        ),
        name="frame_attention",
    )(
        row(token_session), frames, row(ln_gain), w_key, w_value, row(k_bias), row(v_bias), queries, cache_key,
        cache_value, cache_start, cache_len,
    )


def solution(mesh):
    rows = ("grp", "seq")
    return jax.shard_map(
        local,
        mesh=mesh,
        in_specs=(
            P(rows, "mp"), P(rows), P("mp"), P("mp", None), P("mp", None), P("mp"), P("mp"), P(rows, "mp"),
            P(rows, None, "mp"), P(rows, None, "mp"), P(rows), P(rows),
        ),
        out_specs=P(rows, "mp"),
        check_vma=False,
    )
```

time: 77.6 us -> 35.7 us (0.46)
  Pallas kernels: 0 us -> 34.2 us
  starting transfers between devices: 27.5 us -> 0 us
  waiting for transfers between devices: 24.2 us -> 0 us
  local copies, waits for them, and re-layouts: 9.28 us -> 1.38 us
  matrix products: 5.54 us -> 0 us
  other arithmetic: 5.37 us -> 0 us
  blocking collectives: 4.32 us -> 0 us
  between operations: 1.01 us -> 0.01 us
    pallas_call x0 -> x1, Pallas kernels: none -> 34.2 us  [local(): pl.pallas_call(kernel, out_shape=jax.ShapeDtypeStruct(queries.shape, BF16...]
    all_to_all x3 -> x0, starting transfers between devices: 27.5 us -> none  [the longest x1 18.1 us: local(): lax.all_to_all(session_slots, ('grp', 'seq'), split_axis=0, concat_axis=0...]
    all_to_all x3 -> x0, waiting for transfers between devices: 24.2 us -> none  [the longest x1 14.6 us: in_one_piece(): lax.all_to_all(both, axis, split_axis=split_dim, concat_axis=concat_dim,...]
    dot_general x6 -> x0, matrix products: 5.54 us -> none  [the longest x1 3.44 us: project(): part_value = jnp.dot(normed, w_value, preferred_element_type=jnp.float32)]
    gather x6 -> x0, local copies, waits for them, and re-layouts: 4.42 us -> none  [the longest x2 2 us: slot_sources(): sessions = jnp.where(filled, jnp.mod(token_session[source], per_shard), -1)]
    unnamed x1 -> x0, blocking collectives: 4.32 us -> none
    reduce_sum x7 -> x0, other arithmetic: 2.11 us -> none  [the longest x1 1.44 us: project(): partial_squares = jnp.sum(values32 * values32, axis=1)]
    unnamed x26 -> x1, local copies, waits for them, and re-layouts: 2.65 us -> 1.38 us
  transfers between devices with their start and end apart: 3 -> 0, of which waited for: 3 -> 0; matrix products, arithmetic and copies ran while one was open for 12% -> 0% of each run, Pallas kernels for 0% -> 0%
where the time goes in v1:
time: 35.7 us; the launch traced here: 35.6 us
  Pallas kernels  34.2 us (96%)
  local copies, waits for them, and re-layouts  1.38 us (4%)
    pallas_call x1, Pallas kernels, local(): pl.pallas_call(kernel, out_shape=jax.ShapeDtypeStruct(queries.shape, BF16...  34.2 us
    unnamed x1, local copies, waits for them, and re-layouts  1.38 us

profile of v1, /device:TPU:1, one launch (start us, length us, event | category | flops | bytes accessed | tf_op | source)
XLA Modules:
  0.0 35.6 jit_solution(8696519819937157627)
XLA Ops:
  0.0 34.2 %frame_attention.1 = bf16[8,2048]{1,0:T(8,128)(2,1)} custom-call(s32[1,96]{1,0:T(1,128)} %bitcast.7, bf16[96,4096]{1,0:T(8,128)(2,1)} %frames_hbm.1, f32[1,4096]{1,0:T(1,128)} %bitcast.4, bf16[4096,512]{1,0:T(8,128)(2,1)} %wk_hbm.1, bf16[4096,512]{1,0:T(8,128)(2,1)} %wv_hbm.1, f32[1,256]{1,0:T(1,128)} %bitcast.5, f32[1,256]{1,0:T(1,128)} %bitcast.6, ...), custom_call_target="tpu_custom_call" | custom-call | tf_op jit(solution)/shard_map/frame_attention/pallas_call | solution.py:282
  34.2 1.4 %copy.14 = bf16[8,2048]{1,0:T(8,128)(2,1)} copy(bf16[8,2048]{1,0:T(8,128)(2,1)} %frame_attention.1) | data formatting | bytes 65536

commit v2 on v1

--- a/solution.py
+++ b/solution.py
@@ -22,24 +22,24 @@
     tok_hbm, frames_hbm, gain_hbm, wk_hbm, wv_hbm, kb_hbm, vb_hbm, q_hbm, ck_hbm, cv_hbm, start_hbm, len_hbm,
     out_ref,
     tok, frames, gain, weights, kb, vb, q, ck, cv, start, length,
-    normed, square_out, square_in, part_out, part_in, own_part, onehot, send, recv, send_id, recv_id, cached,
-    sem_in, sem_w, sem_sq, sem_part_s, sem_part_r, sem_data, sem_id, know1, know2, know3,
+    normed, square_out, square_in, part_out, part_in, own_part, onehot, send, recv, line_tok, all_tok, cached,
+    sem_in, sem_w, sem_sq, sem_part_s, sem_part_r, sem_data, sem_line, sem_all, know1, know2, know3,
 ):
     g, s, m = lax.axis_index("grp"), lax.axis_index("seq"), lax.axis_index("mp")
     core, y, z = lax.rem(s, NC), lax.rem(s // NC, NY), s // (NC * NY)
     me = g * (NZ * NY * NC) + s
+    column = (g * NY + y) * NC + core
     rows, depth = frames.shape
     half = kb.shape[1]
-
-    def seq_of(zz, yy, cc):
-        return zz * (NY * NC) + yy * NC + cc
+    at_g = [g, 1 - g]
+    at_z = [z] + [lax.rem(z + d, NZ) * (NY * NC) for d in range(1, NZ)]
+    at_z[0] = z * (NY * NC)
+    at_y = [y * NC] + [lax.rem(y + d, NY) * NC for d in range(1, NY)]
+    at_core = [core, 1 - core]
+    at_yc = [[at_y[dy] + at_core[dc] for dc in range(NC)] for dy in range(NY)]
 
     def turned(dg, dz, dy, dc):
-        return (
-            lax.rem(g + dg, NG),
-            seq_of(lax.rem(z + dz, NZ), lax.rem(y + dy, NY), lax.rem(core + dc, NC)),
-            m,
-        )
+        return (at_g[dg], at_z[dz] + at_yc[dy][dc], m)
 
     other = (g, s, 1 - m)
 
@@ -48,7 +48,7 @@
             pl.semaphore_signal(sem, inc=1, device_id=device, device_id_type=MESH)
 
     barrier = pltpu.get_barrier_semaphore()
-    far_core = seq_of(z, y, 1 - core)
+    far_core = at_z[0] + at_yc[0][1]
     near = [
         other, (1 - g, s, 1 - m), (g, far_core, 1 - m), (1 - g, far_core, 1 - m), (g, far_core, m),
         turned(0, 1, 0, 0), turned(0, NZ - 1, 0, 0), turned(0, 0, 1, 0), turned(0, 0, NY - 1, 0),
@@ -111,10 +111,10 @@
     tell(know1, [turned(0, 1, 0, 0), turned(0, NZ - 1, 0, 0), turned(0, 0, 1, 0), turned(0, 0, NY - 1, 0), other])
 
     tok_load.wait()
+    padded = jnp.concatenate([tok[...].astype(F32), jnp.full((1, lanes - rows), -8.0 * PARTS, F32)], axis=1)
+    line_tok[z] = padded
     row_at = lax.broadcasted_iota(jnp.int32, (1, lanes), 1)
-    session = jnp.concatenate([tok[...].astype(F32), jnp.full((1, lanes - rows), -8.0 * PARTS, F32)], axis=1)
-    block = jnp.floor(session * 0.125)
-    within = session - block * 8.0
+    block = jnp.floor(padded * 0.125)
     block_here = jnp.broadcast_to(block, (lanes, lanes))
     lane_i = lax.broadcasted_iota(jnp.int32, (lanes, lanes), 1)
     sub_i = lax.broadcasted_iota(jnp.int32, (lanes, lanes), 0)
@@ -122,13 +122,6 @@
     rank = jnp.sum(before.astype(F32), axis=0, keepdims=True)
     slot = jnp.where(row_at < rows, block * 2.0 + rank, -1.0)
     slot_here = jnp.broadcast_to(slot, (lanes, lanes))
-    ids = []
-    for j in range(2):
-        hit = slot_here == (2 * sub_i + j).astype(F32)
-        ids.append(jnp.sum(jnp.where(hit, within + 1.0, 0.0), axis=1, keepdims=True))
-    id_here = jnp.where(lax.rem(lane_i // 4, 2) == 0, ids[0], ids[1])
-    id_here = jnp.where(lane_i // 8 == lax.rem(me, 16), id_here, 0.0)
-    send_id[...] = id_here.reshape(PARTS, 1, lanes)
     for p in range(8):
         big = lax.broadcasted_iota(jnp.int32, (lanes, lanes), 0)
         hit = jnp.broadcast_to(slot, (lanes, lanes)) == (big // 4 + p * 32).astype(F32)
@@ -155,6 +148,10 @@
         turned(dg, 0, dy, dc) for dg in range(NG) for dy in range(NY) for dc in range(NC) if dg or dy or dc
     ]
     tell(know3, group)
+    for d in range(1, NZ):
+        pltpu.make_async_remote_copy(
+            line_tok.at[z], line_tok.at[z], sem_line.at[0], sem_line.at[1], device_id=turned(0, d, 0, 0), device_id_type=MESH
+        ).start()
 
     part_copies = []
     for i in range(4):
@@ -169,23 +166,17 @@
             part_copies.append(copy)
         else:
             own_part[i - 2] = product
+    some = pl.ds(0, NZ - 1)
+    pltpu.make_async_remote_copy(
+        line_tok.at[some], line_tok.at[some], sem_line.at[0], sem_line.at[1], device_id=other, device_id_type=MESH
+    ).wait()
+    for device in group:
+        pltpu.make_async_remote_copy(
+            line_tok, all_tok.at[column], sem_all.at[0], sem_all.at[1], device_id=device, device_id_type=MESH
+        ).start()
+    all_tok[column] = line_tok[...]
     for load in small + late:
         load.wait()
-
-    pl.semaphore_wait(know3, len(group))
-
-    def peer(k):
-        return turned(k // (NZ * NY * NC), lax.rem(k // (NY * NC), NZ), lax.rem(k // NC, NY), lax.rem(k, NC))
-
-    @pl.loop(1, PARTS)
-    def _(k):
-        device = peer(k)
-        to = device[0] * (NZ * NY * NC) + device[1]
-        pltpu.make_async_remote_copy(
-            send_id.at[to], recv_id.at[me], sem_id.at[0], sem_id.at[1], device_id=device, device_id_type=MESH
-        ).start()
-
-    recv_id[me] = send_id[me]
 
     heads = q.shape[1] // HEAD
     kv_heads = heads // GROUP
@@ -218,28 +209,44 @@
     slotted = jnp.dot(onehot[...], table, preferred_element_type=F32).astype(BF16)
     send[...] = slotted.reshape(send.shape)
 
-    @pl.loop(1, PARTS)
-    def _(k):
-        device = peer(k)
-        to = device[0] * (NZ * NY * NC) + device[1]
-        pltpu.make_async_remote_copy(
-            send.at[to], recv.at[me], sem_data.at[0], sem_data.at[1], device_id=device, device_id_type=MESH
-        ).start()
-
-    recv[me] = send[me]
+    pl.semaphore_wait(know3, len(group))
+    here = column * NZ + z
+    for dz in (4, 3, 5, 2, 6, 1, 7, 0):
+        for dg in (1, 0):
+            for dy in (2, 1, 3, 0):
+                for dc in (0, 1):
+                    if dg or dz or dy or dc:
+                        device = turned(dg, dz, dy, dc)
+                        to = device[0] * (NZ * NY * NC) + device[1]
+                        pltpu.make_async_remote_copy(
+                            send.at[to], recv.at[here], sem_data.at[0], sem_data.at[1], device_id=device,
+                            device_id_type=MESH,
+                        ).start()
+    recv[here] = send[me]
+
+    some = pl.ds(0, 15)
+    pltpu.make_async_remote_copy(
+        all_tok.at[some], all_tok.at[some], sem_all.at[0], sem_all.at[1], device_id=other, device_id_type=MESH
+    ).wait()
+    came = all_tok[...].reshape(PARTS, lanes)
+    came_block = jnp.floor(came * 0.125)
+    mine = came_block == jnp.full((1, 1), me, jnp.int32).astype(F32)
+    upto = jnp.where(sub_i <= lane_i, 1.0, 0.0).astype(BF16)
+    rank = jnp.dot(jnp.where(mine, 1.0, 0.0).astype(BF16), upto, preferred_element_type=F32)
+    name = jnp.where(mine, came - came_block * 8.0 + 1.0, 0.0)
+    first = jnp.sum(jnp.where(rank == 1.0, name, 0.0), axis=1, keepdims=True)
+    second = jnp.sum(jnp.where(rank == 2.0, name, 0.0), axis=1, keepdims=True)
+    names = jnp.where(lax.rem(lane_i // 4, 2) == 0, first, second)
+    names = jnp.where(lane_i // 8 == lax.rem(sub_i, 16), names, 0.0)
+    names = [jnp.sum(names[16 * i : 16 * i + 16], axis=0, keepdims=True) for i in range(8)]
+    ids_row = jnp.concatenate(names, axis=1)
 
     everyone = pl.ds(0, PARTS - 1)
-    pltpu.make_async_remote_copy(
-        send_id.at[everyone], recv_id.at[everyone], sem_id.at[0], sem_id.at[1], device_id=other, device_id_type=MESH
-    ).wait()
-    lane_ids = [jnp.sum(recv_id[pl.ds(16 * i, 16)], axis=0) for i in range(8)]
     pltpu.make_async_remote_copy(
         send.at[everyone], recv.at[everyone], sem_data.at[0], sem_data.at[1], device_id=other, device_id_type=MESH
     ).wait()
-
     fresh_rows = recv[...].reshape(PARTS * 8, HEAD)
     fresh = lax.dot_general(stacked, fresh_rows, (((1,), (1,)), ((), ())), preferred_element_type=F32) * scale
-    ids_row = jnp.concatenate(lane_ids, axis=1)
     shape = fresh.shape
     row_i = lax.broadcasted_iota(jnp.int32, shape, 0)
     col_i = lax.broadcasted_iota(jnp.int32, shape, 1)
@@ -290,9 +297,9 @@
             vm(cache_value.shape, BF16), pltpu.SMEM((8,), jnp.int32), pltpu.SMEM((8,), jnp.int32),
             vm((rows, depth), BF16), vm((1, 128), F32), vm((1, 128), F32), vm((2, rows, half), F32),
             vm((2, rows, half), F32), vm((2, rows, half), F32), vm((PARTS * 8, 512), BF16),
-            vm((PARTS, 8, HEAD), BF16), vm((PARTS, 8, HEAD), BF16), vm((PARTS, 1, 128), F32), vm((PARTS, 1, 128), F32),
+            vm((PARTS, 8, HEAD), BF16), vm((PARTS, 8, HEAD), BF16), vm((NZ, 1, 128), F32), vm((16, NZ, 1, 128), F32),
             vm((128, 128), F32),
-            dma((16,)), dma((4,)), dma((2,)), dma((2,)), dma((2,)), dma((2,)), dma((2,)),
+            dma((16,)), dma((4,)), dma((2,)), dma((2,)), dma((2,)), dma((2,)), dma((2,)), dma((2,)),
             regular, regular, regular,
         ],
         compiler_params=pltpu.CompilerParams(

time: 35.7 us -> 32 us (0.90)
  Pallas kernels: 34.2 us -> 30.5 us
    pallas_call x1, Pallas kernels: 34.2 us -> 30.5 us  [local(): pl.pallas_call(kernel, out_shape=jax.ShapeDtypeStruct(queries.shape, BF16...]
where the time goes in v2:
time: 32 us; the launch traced here: 31.9 us
  Pallas kernels  30.5 us (95%)
  local copies, waits for them, and re-layouts  1.38 us (4%)
    pallas_call x1, Pallas kernels, local(): pl.pallas_call(kernel, out_shape=jax.ShapeDtypeStruct(queries.shape, BF16...  30.5 us
    unnamed x1, local copies, waits for them, and re-layouts  1.38 us

profile of v2, /device:TPU:1, one launch (start us, length us, event | category | flops | bytes accessed | tf_op | source)
XLA Modules:
  0.0 31.9 jit_solution(5852890989102852315)
XLA Ops:
  0.0 30.5 %frame_attention.1 = bf16[8,2048]{1,0:T(8,128)(2,1)} custom-call(s32[1,96]{1,0:T(1,128)} %bitcast.7, bf16[96,4096]{1,0:T(8,128)(2,1)} %frames_hbm.1, f32[1,4096]{1,0:T(1,128)} %bitcast.4, bf16[4096,512]{1,0:T(8,128)(2,1)} %wk_hbm.1, bf16[4096,512]{1,0:T(8,128)(2,1)} %wv_hbm.1, f32[1,256]{1,0:T(1,128)} %bitcast.5, f32[1,256]{1,0:T(1,128)} %bitcast.6, ...), custom_call_target="tpu_custom_call" | custom-call | tf_op jit(solution)/shard_map/frame_attention/pallas_call | solution.py:289
  30.5 1.4 %copy.14 = bf16[8,2048]{1,0:T(8,128)(2,1)} copy(bf16[8,2048]{1,0:T(8,128)(2,1)} %frame_attention.1) | data formatting | bytes 65536

commit v3 on v2

--- a/solution.py
+++ b/solution.py
@@ -23,7 +23,7 @@
     out_ref,
     tok, frames, gain, weights, kb, vb, q, ck, cv, start, length,
     normed, square_out, square_in, part_out, part_in, own_part, onehot, send, recv, line_tok, all_tok, cached,
-    sem_in, sem_w, sem_sq, sem_part_s, sem_part_r, sem_data, sem_line, sem_all, know1, know2, know3,
+    sem_in, sem_w, sem_sq, sem_part_s, sem_part_r, sem_data_s, sem_data_r, sem_line, sem_all, know1, know2, know3,
 ):
     g, s, m = lax.axis_index("grp"), lax.axis_index("seq"), lax.axis_index("mp")
     core, y, z = lax.rem(s, NC), lax.rem(s // NC, NY), s // (NC * NY)
@@ -122,12 +122,11 @@
     rank = jnp.sum(before.astype(F32), axis=0, keepdims=True)
     slot = jnp.where(row_at < rows, block * 2.0 + rank, -1.0)
     slot_here = jnp.broadcast_to(slot, (lanes, lanes))
-    for p in range(8):
-        big = lax.broadcasted_iota(jnp.int32, (lanes, lanes), 0)
-        hit = jnp.broadcast_to(slot, (lanes, lanes)) == (big // 4 + p * 32).astype(F32)
-        for c in range(4):
-            onehot[pl.ds(p * lanes, lanes), pl.ds(c * lanes, lanes)] = jnp.where(
-                hit & (lax.rem(big, 4) == c), 1.0, 0.0
+    for p in range(4):
+        hit = slot_here == (sub_i // 2 + p * 64).astype(F32)
+        for h in range(2):
+            onehot[pl.ds(p * lanes, lanes), pl.ds(h * lanes, lanes)] = jnp.where(
+                hit & (lax.rem(sub_i, 2) == h), 1.0, 0.0
             ).astype(BF16)
 
     pl.semaphore_wait(know1, 5)
@@ -166,15 +165,6 @@
             part_copies.append(copy)
         else:
             own_part[i - 2] = product
-    some = pl.ds(0, NZ - 1)
-    pltpu.make_async_remote_copy(
-        line_tok.at[some], line_tok.at[some], sem_line.at[0], sem_line.at[1], device_id=other, device_id_type=MESH
-    ).wait()
-    for device in group:
-        pltpu.make_async_remote_copy(
-            line_tok, all_tok.at[column], sem_all.at[0], sem_all.at[1], device_id=device, device_id_type=MESH
-        ).start()
-    all_tok[column] = line_tok[...]
     for load in small + late:
         load.wait()
 
@@ -198,31 +188,42 @@
             score = jnp.where(row_session == b, product, score)
         cached[pl.ds(h * GROUP * per_shard, GROUP * per_shard)] = score
 
-    parts = []
+    here = column * NZ + z
+    peers = [
+        (dg, dz, dy, dc)
+        for dz in (4, 3, 5, 2, 6, 1, 7, 0) for dg in (1, 0) for dy in (2, 1, 3, 0) for dc in (0, 1)
+        if dg or dz or dy or dc
+    ]
     for i, bias in enumerate((kb, vb)):
         part_copies[i].wait()
         whole = (own_part[i] + part_in[i] + bias[...]).astype(BF16)
+        parts = []
         for h in range(kv_heads):
             parts.append(whole[:, h * HEAD : (h + 1) * HEAD])
             parts.append(jnp.zeros((lanes - rows, HEAD), BF16))
-    table = jnp.concatenate(parts, axis=0)
-    slotted = jnp.dot(onehot[...], table, preferred_element_type=F32).astype(BF16)
-    send[...] = slotted.reshape(send.shape)
-
-    pl.semaphore_wait(know3, len(group))
-    here = column * NZ + z
-    for dz in (4, 3, 5, 2, 6, 1, 7, 0):
-        for dg in (1, 0):
-            for dy in (2, 1, 3, 0):
-                for dc in (0, 1):
-                    if dg or dz or dy or dc:
-                        device = turned(dg, dz, dy, dc)
-                        to = device[0] * (NZ * NY * NC) + device[1]
-                        pltpu.make_async_remote_copy(
-                            send.at[to], recv.at[here], sem_data.at[0], sem_data.at[1], device_id=device,
-                            device_id_type=MESH,
-                        ).start()
-    recv[here] = send[me]
+        table = jnp.concatenate(parts, axis=0)
+        slotted = jnp.dot(onehot[...], table, preferred_element_type=F32).astype(BF16)
+        send[i] = slotted.reshape(PARTS, 4, HEAD)
+        if i == 0:
+            pl.semaphore_wait(know3, len(group))
+        for turn in peers:
+            device = turned(*turn)
+            to = device[0] * (NZ * NY * NC) + device[1]
+            pltpu.make_async_remote_copy(
+                send.at[i, to], recv.at[i, here], sem_data_s.at[i], sem_data_r.at[i], device_id=device,
+                device_id_type=MESH,
+            ).start()
+        recv[i, here] = send[i, me]
+        if i == 0:
+            some = pl.ds(0, NZ - 1)
+            pltpu.make_async_remote_copy(
+                line_tok.at[some], line_tok.at[some], sem_line.at[0], sem_line.at[1], device_id=other, device_id_type=MESH
+            ).wait()
+            for device in group:
+                pltpu.make_async_remote_copy(
+                    line_tok, all_tok.at[column], sem_all.at[0], sem_all.at[1], device_id=device, device_id_type=MESH
+                ).start()
+            all_tok[column] = line_tok[...]
 
     some = pl.ds(0, 15)
     pltpu.make_async_remote_copy(
@@ -236,22 +237,25 @@
     name = jnp.where(mine, came - came_block * 8.0 + 1.0, 0.0)
     first = jnp.sum(jnp.where(rank == 1.0, name, 0.0), axis=1, keepdims=True)
     second = jnp.sum(jnp.where(rank == 2.0, name, 0.0), axis=1, keepdims=True)
-    names = jnp.where(lax.rem(lane_i // 4, 2) == 0, first, second)
-    names = jnp.where(lane_i // 8 == lax.rem(sub_i, 16), names, 0.0)
-    names = [jnp.sum(names[16 * i : 16 * i + 16], axis=0, keepdims=True) for i in range(8)]
+    names = jnp.where(lax.rem(lane_i // 2, 2) == 0, first, second)
+    names = jnp.where(lane_i // 4 == lax.rem(sub_i, 32), names, 0.0)
+    names = [jnp.sum(names[32 * i : 32 * i + 32], axis=0, keepdims=True) for i in range(4)]
     ids_row = jnp.concatenate(names, axis=1)
 
-    everyone = pl.ds(0, PARTS - 1)
-    pltpu.make_async_remote_copy(
-        send.at[everyone], recv.at[everyone], sem_data.at[0], sem_data.at[1], device_id=other, device_id_type=MESH
-    ).wait()
-    fresh_rows = recv[...].reshape(PARTS * 8, HEAD)
-    fresh = lax.dot_general(stacked, fresh_rows, (((1,), (1,)), ((), ())), preferred_element_type=F32) * scale
+    def arrived(i):
+        everyone = pl.ds(0, PARTS - 1)
+        pltpu.make_async_remote_copy(
+            send.at[i, everyone], recv.at[i, everyone], sem_data_s.at[i], sem_data_r.at[i], device_id=other,
+            device_id_type=MESH,
+        ).wait()
+        return recv[i].reshape(PARTS * 4, HEAD)
+
+    fresh = lax.dot_general(stacked, arrived(0), (((1,), (1,)), ((), ())), preferred_element_type=F32) * scale
     shape = fresh.shape
     row_i = lax.broadcasted_iota(jnp.int32, shape, 0)
     col_i = lax.broadcasted_iota(jnp.int32, shape, 1)
     match = (ids_row == (lax.rem(row_i, per_shard) + 1).astype(F32)) & (
-        lax.rem(col_i, 4) == row_i // (GROUP * per_shard)
+        lax.rem(col_i, 2) == row_i // (GROUP * per_shard)
     )
     fresh = jnp.where(match, fresh, -jnp.inf)
     held = cached[...]
@@ -261,18 +265,20 @@
     total = jnp.sum(held_exp, axis=1, keepdims=True) + jnp.sum(fresh_exp, axis=1, keepdims=True)
     inverse_total = 1.0 / total
     held_weights = held_exp * inverse_total
-    fresh_weights = pltpu.roll(fresh_exp * inverse_total, 2, 1).astype(BF16)
-    result = jnp.dot(fresh_weights, fresh_rows, preferred_element_type=F32)
+    fresh_weights = (fresh_exp * inverse_total).astype(BF16)
+    held_terms = []
     for h in range(kv_heads):
-        part = result[h * GROUP * per_shard : (h + 1) * GROUP * per_shard]
         mine = held_weights[h * GROUP * per_shard : (h + 1) * GROUP * per_shard]
+        part = jnp.zeros((GROUP * per_shard, HEAD), F32)
         for b in range(per_shard):
             only = jnp.where(row_session == b, mine, 0.0).astype(BF16)
             part = part + jnp.dot(only, cv[b, :, pl.ds(h * HEAD, HEAD)], preferred_element_type=F32)
-        for i in range(GROUP):
-            out_ref[:, pl.ds((h * GROUP + i) * HEAD, HEAD)] = part[
-                i * per_shard : (i + 1) * per_shard
-            ].astype(BF16)
+        held_terms.append(part)
+    held_terms = jnp.concatenate(held_terms, axis=0)
+
+    result = held_terms + jnp.dot(fresh_weights, arrived(1), preferred_element_type=F32)
+    for i in range(heads):
+        out_ref[:, pl.ds(i * HEAD, HEAD)] = result[i * per_shard : (i + 1) * per_shard].astype(BF16)
 
 
 def local(
@@ -296,10 +302,10 @@
             vm((1, half), F32), vm((1, half), F32), vm(queries.shape, BF16), vm(cache_key.shape, BF16),
             vm(cache_value.shape, BF16), pltpu.SMEM((8,), jnp.int32), pltpu.SMEM((8,), jnp.int32),
             vm((rows, depth), BF16), vm((1, 128), F32), vm((1, 128), F32), vm((2, rows, half), F32),
-            vm((2, rows, half), F32), vm((2, rows, half), F32), vm((PARTS * 8, 512), BF16),
-            vm((PARTS, 8, HEAD), BF16), vm((PARTS, 8, HEAD), BF16), vm((NZ, 1, 128), F32), vm((16, NZ, 1, 128), F32),
+            vm((2, rows, half), F32), vm((2, rows, half), F32), vm((PARTS * 4, 256), BF16),
+            vm((2, PARTS, 4, HEAD), BF16), vm((2, PARTS, 4, HEAD), BF16), vm((NZ, 1, 128), F32), vm((16, NZ, 1, 128), F32),
             vm((128, 128), F32),
-            dma((16,)), dma((4,)), dma((2,)), dma((2,)), dma((2,)), dma((2,)), dma((2,)), dma((2,)),
+            dma((16,)), dma((4,)), dma((2,)), dma((2,)), dma((2,)), dma((2,)), dma((2,)), dma((2,)), dma((2,)),
             regular, regular, regular,
         ],
         compiler_params=pltpu.CompilerParams(

time: 32 us -> 30 us (0.938)
  Pallas kernels: 30.5 us -> 28.4 us
    pallas_call x1, Pallas kernels: 30.5 us -> 28.4 us  [local(): pl.pallas_call(kernel, out_shape=jax.ShapeDtypeStruct(queries.shape, BF16...]
where the time goes in v3:
time: 30 us; the launch traced here: 29.8 us
  Pallas kernels  28.4 us (95%)
  local copies, waits for them, and re-layouts  1.38 us (5%)
    pallas_call x1, Pallas kernels, local(): pl.pallas_call(kernel, out_shape=jax.ShapeDtypeStruct(queries.shape, BF16...  28.4 us
    unnamed x1, local copies, waits for them, and re-layouts  1.38 us

profile of v3, /device:TPU:1, one launch (start us, length us, event | category | flops | bytes accessed | tf_op | source)
XLA Modules:
  0.0 29.8 jit_solution(8862977381892644255)
XLA Ops:
  0.0 28.4 %frame_attention.1 = bf16[8,2048]{1,0:T(8,128)(2,1)} custom-call(s32[1,96]{1,0:T(1,128)} %bitcast.7, bf16[96,4096]{1,0:T(8,128)(2,1)} %frames_hbm.1, f32[1,4096]{1,0:T(1,128)} %bitcast.4, bf16[4096,512]{1,0:T(8,128)(2,1)} %wk_hbm.1, bf16[4096,512]{1,0:T(8,128)(2,1)} %wv_hbm.1, f32[1,256]{1,0:T(1,128)} %bitcast.5, f32[1,256]{1,0:T(1,128)} %bitcast.6, ...), custom_call_target="tpu_custom_call" | custom-call | tf_op jit(solution)/shard_map/frame_attention/pallas_call | solution.py:295
  28.5 1.4 %copy.14 = bf16[8,2048]{1,0:T(8,128)(2,1)} copy(bf16[8,2048]{1,0:T(8,128)(2,1)} %frame_attention.1) | data formatting | bytes 65536

commit v4 on v3

--- a/solution.py
+++ b/solution.py
@@ -90,6 +90,9 @@
     for load in small + late:
         load.start()
 
+    pl.semaphore_wait(barrier, len(near))
+    tell(know1, [turned(0, 1, 0, 0), turned(0, NZ - 1, 0, 0), turned(0, 0, 1, 0), turned(0, 0, NY - 1, 0), other])
+
     lanes = 128
     square_out[...] = jnp.zeros_like(square_out)
     sums = []
@@ -103,12 +106,13 @@
     sums.append(jnp.zeros((lanes - rows, lanes), F32))
     own_squares = jnp.sum(jnp.concatenate(sums, axis=0).T, axis=0, keepdims=True)
     square_out[...] = own_squares
-    pl.semaphore_wait(barrier, len(near))
     square_copy = pltpu.make_async_remote_copy(
         square_out, square_in, sem_sq.at[0], sem_sq.at[1], device_id=other, device_id_type=MESH
     )
     square_copy.start()
-    tell(know1, [turned(0, 1, 0, 0), turned(0, NZ - 1, 0, 0), turned(0, 0, 1, 0), turned(0, 0, NY - 1, 0), other])
+    pl.semaphore_wait(know1, 5)
+    line = [turned(0, 0, d, 0) for d in range(1, NY)]
+    tell(know2, [turned(0, 2, 0, 0), turned(0, NZ - 2, 0, 0)] + line)
 
     tok_load.wait()
     padded = jnp.concatenate([tok[...].astype(F32), jnp.full((1, lanes - rows), -8.0 * PARTS, F32)], axis=1)
@@ -129,42 +133,54 @@
                 hit & (lax.rem(sub_i, 2) == h), 1.0, 0.0
             ).astype(BF16)
 
-    pl.semaphore_wait(know1, 5)
-    line = [turned(0, 0, d, 0) for d in range(1, NY)]
-    tell(know2, [turned(0, 2, 0, 0), turned(0, NZ - 2, 0, 0)] + line)
+    pl.semaphore_wait(know2, 5)
+    group = [
+        turned(dg, 0, dy, dc) for dg in range(NG) for dy in range(NY) for dc in range(NC) if dg or dy or dc
+    ]
+    tell(know3, group)
+    for d in range(1, NZ):
+        pltpu.make_async_remote_copy(
+            line_tok.at[z], line_tok.at[z], sem_line.at[0], sem_line.at[1], device_id=turned(0, d, 0, 0), device_id_type=MESH
+        ).start()
 
     gain_load.wait()
     square_copy.wait()
     squares = square_out[...] + square_in[...]
     inverse = lax.rsqrt(squares / (2 * depth) + EPSILON)
     inverse = jnp.broadcast_to(inverse, (lanes, lanes)).T[:rows]
-    for j in range(depth // lanes):
-        cols = pl.ds(j * lanes, lanes)
-        normed[:, cols] = (frames[:, cols].astype(F32) * inverse * gain[:, cols]).astype(BF16)
-
-    pl.semaphore_wait(know2, 5)
-    group = [
-        turned(dg, 0, dy, dc) for dg in range(NG) for dy in range(NY) for dc in range(NC) if dg or dy or dc
-    ]
-    tell(know3, group)
-    for d in range(1, NZ):
-        pltpu.make_async_remote_copy(
-            line_tok.at[z], line_tok.at[z], sem_line.at[0], sem_line.at[1], device_id=turned(0, d, 0, 0), device_id_type=MESH
-        ).start()
-
-    part_copies = []
-    for i in range(4):
+    step = 512
+    first_product = jnp.zeros((rows, half), F32)
+    weight_loads[0].wait()
+    for j in range(depth // step):
+        cols = pl.ds(j * step, step)
+        chunk_normed = (frames[:, cols].astype(F32) * inverse[:, :1] * gain[:, cols]).astype(BF16)
+        normed[:, cols] = chunk_normed
+        first_product = first_product + jnp.dot(chunk_normed, weights[0, cols], preferred_element_type=F32)
+
+    part_copies, top_copies = [], []
+    split = part_out.shape[0] // 2
+    width = half // split
+
+    def share(product, i):
+        for at in range(split):
+            piece = product[:, at * width : (at + 1) * width]
+            j = i * split + at
+            part_out[j] = piece
+            copy = pltpu.make_async_remote_copy(
+                part_out.at[j], part_in.at[j], sem_part_s.at[j], sem_part_r.at[j], device_id=other, device_id_type=MESH
+            )
+            copy.start()
+            part_copies.append(copy)
+
+    share(first_product, 0)
+    for i in range(1, 4):
         weight_loads[i].wait()
         product = jnp.dot(normed[...], weights[i], preferred_element_type=F32)
         if i < 2:
-            part_out[i] = product
-            copy = pltpu.make_async_remote_copy(
-                part_out.at[i], part_in.at[i], sem_part_s.at[i], sem_part_r.at[i], device_id=other, device_id_type=MESH
-            )
-            copy.start()
-            part_copies.append(copy)
+            share(product, i)
         else:
-            own_part[i - 2] = product
+            for at in range(split):
+                own_part[(i - 2) * split + at] = product[:, at * width : (at + 1) * width]
     for load in small + late:
         load.wait()
 
@@ -194,16 +210,17 @@
         for dz in (4, 3, 5, 2, 6, 1, 7, 0) for dg in (1, 0) for dy in (2, 1, 3, 0) for dc in (0, 1)
         if dg or dz or dy or dc
     ]
-    for i, bias in enumerate((kb, vb)):
+    for i in range(2 * split):
+        bias = (kb, vb)[i // split][:, (i % split) * width : (i % split + 1) * width]
         part_copies[i].wait()
-        whole = (own_part[i] + part_in[i] + bias[...]).astype(BF16)
+        whole = (own_part[i] + part_in[i] + bias).astype(BF16)
         parts = []
-        for h in range(kv_heads):
+        for h in range(width // HEAD):
             parts.append(whole[:, h * HEAD : (h + 1) * HEAD])
             parts.append(jnp.zeros((lanes - rows, HEAD), BF16))
         table = jnp.concatenate(parts, axis=0)
         slotted = jnp.dot(onehot[...], table, preferred_element_type=F32).astype(BF16)
-        send[i] = slotted.reshape(PARTS, 4, HEAD)
+        send[i] = slotted.reshape(send.shape[1:])
         if i == 0:
             pl.semaphore_wait(know3, len(group))
         for turn in peers:
@@ -214,7 +231,7 @@
                 device_id_type=MESH,
             ).start()
         recv[i, here] = send[i, me]
-        if i == 0:
+        if i == split - 1:
             some = pl.ds(0, NZ - 1)
             pltpu.make_async_remote_copy(
                 line_tok.at[some], line_tok.at[some], sem_line.at[0], sem_line.at[1], device_id=other, device_id_type=MESH
@@ -294,7 +311,7 @@
     vm = pltpu.VMEM
     return pl.pallas_call(
         kernel,
-        out_shape=jax.ShapeDtypeStruct(queries.shape, BF16),
+        out_shape=pltpu.VMEM(queries.shape, BF16),
         in_specs=[anywhere] * 12,
         out_specs=pl.BlockSpec(memory_space=pltpu.VMEM),
         scratch_shapes=[
@@ -309,7 +326,7 @@
             regular, regular, regular,
         ],
         compiler_params=pltpu.CompilerParams(
-            collective_id=0, has_side_effects=True, vmem_limit_bytes=67_000_000
+            collective_id=0, has_side_effects=True, vmem_limit_bytes=66_900_000
         ),
         name="frame_attention",
     )(

time: 30 us -> 28.2 us (0.940)
  Pallas kernels: 28.4 us -> 27.5 us
  local copies, waits for them, and re-layouts: 1.38 us -> 0.62 us
    pallas_call x1, Pallas kernels: 28.4 us -> 27.5 us  [local(): pl.pallas_call(kernel, out_shape=pltpu.VMEM(queries.shape, BF16), in_spec...]
    unnamed x1, local copies, waits for them, and re-layouts: 1.38 us -> 0.62 us
where the time goes in v4:
time: 28.2 us
  Pallas kernels  27.5 us (98%)
  local copies, waits for them, and re-layouts  0.62 us (2%)
    pallas_call x1, Pallas kernels, local(): pl.pallas_call(kernel, out_shape=pltpu.VMEM(queries.shape, BF16), in_spec...  27.5 us
    unnamed x1, local copies, waits for them, and re-layouts  0.62 us

profile of v4, /device:TPU:1, one launch (start us, length us, event | category | flops | bytes accessed | tf_op | source)
XLA Modules:
  0.0 28.2 jit_solution(249914016432516722)
XLA Ops:
  0.0 27.5 %frame_attention.1 = bf16[8,2048]{1,0:T(8,128)(2,1)S(1)} custom-call(s32[1,96]{1,0:T(1,128)} %bitcast.7, bf16[96,4096]{1,0:T(8,128)(2,1)} %frames_hbm.1, f32[1,4096]{1,0:T(1,128)} %bitcast.4, bf16[4096,512]{1,0:T(8,128)(2,1)} %wk_hbm.1, bf16[4096,512]{1,0:T(8,128)(2,1)} %wv_hbm.1, f32[1,256]{1,0:T(1,128)} %bitcast.5, f32[1,256]{1,0:T(1,128)} %bitcast.6, ...), custom_call_target="tpu_custom_call" | custom-call | tf_op jit(solution)/shard_map/frame_attention/pallas_call | solution.py:312
  27.6 0.6 %copy.14 = bf16[8,2048]{1,0:T(8,128)(2,1)} copy(bf16[8,2048]{1,0:T(8,128)(2,1)S(1)} %frame_attention.1) | data formatting | bytes 65536

commit v5 on v4

--- a/solution.py
+++ b/solution.py
@@ -23,7 +23,7 @@
     out_ref,
     tok, frames, gain, weights, kb, vb, q, ck, cv, start, length,
     normed, square_out, square_in, part_out, part_in, own_part, onehot, send, recv, line_tok, all_tok, cached,
-    sem_in, sem_w, sem_sq, sem_part_s, sem_part_r, sem_data_s, sem_data_r, sem_line, sem_all, know1, know2, know3,
+    sem_in, sem_w, sem_sq, sem_part_s, sem_part_r, sem_data_s, sem_data_r, sem_line, sem_all, know1, know2,
 ):
     g, s, m = lax.axis_index("grp"), lax.axis_index("seq"), lax.axis_index("mp")
     core, y, z = lax.rem(s, NC), lax.rem(s // NC, NY), s // (NC * NY)
@@ -48,11 +48,9 @@
             pl.semaphore_signal(sem, inc=1, device_id=device, device_id_type=MESH)
 
     barrier = pltpu.get_barrier_semaphore()
-    far_core = at_z[0] + at_yc[0][1]
-    near = [
-        other, (1 - g, s, 1 - m), (g, far_core, 1 - m), (1 - g, far_core, 1 - m), (g, far_core, m),
-        turned(0, 1, 0, 0), turned(0, NZ - 1, 0, 0), turned(0, 0, 1, 0), turned(0, 0, NY - 1, 0),
-    ]
+    near = [other] + [turned(0, d, 0, 0) for d in (1, 2, NZ - 2, NZ - 1)]
+    near += [turned(0, 0, dy, dc) for dy in range(NY) for dc in range(NC) if dy or dc]
+    near += [turned(1, 0, 0, dc) for dc in range(NC)]
     tell(barrier, near)
 
     chunk = 32
@@ -90,9 +88,6 @@
     for load in small + late:
         load.start()
 
-    pl.semaphore_wait(barrier, len(near))
-    tell(know1, [turned(0, 1, 0, 0), turned(0, NZ - 1, 0, 0), turned(0, 0, 1, 0), turned(0, 0, NY - 1, 0), other])
-
     lanes = 128
     square_out[...] = jnp.zeros_like(square_out)
     sums = []
@@ -106,13 +101,12 @@
     sums.append(jnp.zeros((lanes - rows, lanes), F32))
     own_squares = jnp.sum(jnp.concatenate(sums, axis=0).T, axis=0, keepdims=True)
     square_out[...] = own_squares
+    pl.semaphore_wait(barrier, len(near))
     square_copy = pltpu.make_async_remote_copy(
         square_out, square_in, sem_sq.at[0], sem_sq.at[1], device_id=other, device_id_type=MESH
     )
     square_copy.start()
-    pl.semaphore_wait(know1, 5)
-    line = [turned(0, 0, d, 0) for d in range(1, NY)]
-    tell(know2, [turned(0, 2, 0, 0), turned(0, NZ - 2, 0, 0)] + line)
+    tell(know1, [turned(0, 2, 0, 0), turned(0, NZ - 2, 0, 0)] + [turned(0, 0, d, 0) for d in range(1, NY)])
 
     tok_load.wait()
     padded = jnp.concatenate([tok[...].astype(F32), jnp.full((1, lanes - rows), -8.0 * PARTS, F32)], axis=1)
@@ -133,11 +127,11 @@
                 hit & (lax.rem(sub_i, 2) == h), 1.0, 0.0
             ).astype(BF16)
 
-    pl.semaphore_wait(know2, 5)
+    pl.semaphore_wait(know1, 5)
     group = [
         turned(dg, 0, dy, dc) for dg in range(NG) for dy in range(NY) for dc in range(NC) if dg or dy or dc
     ]
-    tell(know3, group)
+    tell(know2, group)
     for d in range(1, NZ):
         pltpu.make_async_remote_copy(
             line_tok.at[z], line_tok.at[z], sem_line.at[0], sem_line.at[1], device_id=turned(0, d, 0, 0), device_id_type=MESH
@@ -204,6 +198,16 @@
             score = jnp.where(row_session == b, product, score)
         cached[pl.ds(h * GROUP * per_shard, GROUP * per_shard)] = score
 
+    some = pl.ds(0, NZ - 1)
+    pltpu.make_async_remote_copy(
+        line_tok.at[some], line_tok.at[some], sem_line.at[0], sem_line.at[1], device_id=other, device_id_type=MESH
+    ).wait()
+    for device in group:
+        pltpu.make_async_remote_copy(
+            line_tok, all_tok.at[column], sem_all.at[0], sem_all.at[1], device_id=device, device_id_type=MESH
+        ).start()
+    all_tok[column] = line_tok[...]
+
     here = column * NZ + z
     peers = [
         (dg, dz, dy, dc)
@@ -222,7 +226,7 @@
         slotted = jnp.dot(onehot[...], table, preferred_element_type=F32).astype(BF16)
         send[i] = slotted.reshape(send.shape[1:])
         if i == 0:
-            pl.semaphore_wait(know3, len(group))
+            pl.semaphore_wait(know2, len(group))
         for turn in peers:
             device = turned(*turn)
             to = device[0] * (NZ * NY * NC) + device[1]
@@ -231,16 +235,6 @@
                 device_id_type=MESH,
             ).start()
         recv[i, here] = send[i, me]
-        if i == split - 1:
-            some = pl.ds(0, NZ - 1)
-            pltpu.make_async_remote_copy(
-                line_tok.at[some], line_tok.at[some], sem_line.at[0], sem_line.at[1], device_id=other, device_id_type=MESH
-            ).wait()
-            for device in group:
-                pltpu.make_async_remote_copy(
-                    line_tok, all_tok.at[column], sem_all.at[0], sem_all.at[1], device_id=device, device_id_type=MESH
-                ).start()
-            all_tok[column] = line_tok[...]
 
     some = pl.ds(0, 15)
     pltpu.make_async_remote_copy(
@@ -323,7 +317,7 @@
             vm((2, PARTS, 4, HEAD), BF16), vm((2, PARTS, 4, HEAD), BF16), vm((NZ, 1, 128), F32), vm((16, NZ, 1, 128), F32),
             vm((128, 128), F32),
             dma((16,)), dma((4,)), dma((2,)), dma((2,)), dma((2,)), dma((2,)), dma((2,)), dma((2,)), dma((2,)),
-            regular, regular, regular,
+            regular, regular,
         ],
         compiler_params=pltpu.CompilerParams(
             collective_id=0, has_side_effects=True, vmem_limit_bytes=66_900_000

time: 28.2 us -> 27.7 us (0.982)
  Pallas kernels: 27.5 us -> 27 us
    pallas_call x1, Pallas kernels: 27.5 us -> 27 us  [local(): pl.pallas_call(kernel, out_shape=pltpu.VMEM(queries.shape, BF16), in_spec...]
where the time goes in v5:
time: 27.7 us
  Pallas kernels  27 us (97%)
  local copies, waits for them, and re-layouts  0.62 us (2%)
    pallas_call x1, Pallas kernels, local(): pl.pallas_call(kernel, out_shape=pltpu.VMEM(queries.shape, BF16), in_spec...  27 us
    unnamed x1, local copies, waits for them, and re-layouts  0.62 us

profile of v5, /device:TPU:1, one launch (start us, length us, event | category | flops | bytes accessed | tf_op | source)
XLA Modules:
  0.0 27.7 jit_solution(15271643674912616420)
XLA Ops:
  0.0 27.0 %frame_attention.1 = bf16[8,2048]{1,0:T(8,128)(2,1)S(1)} custom-call(s32[1,96]{1,0:T(1,128)} %bitcast.7, bf16[96,4096]{1,0:T(8,128)(2,1)} %frames_hbm.1, f32[1,4096]{1,0:T(1,128)} %bitcast.4, bf16[4096,512]{1,0:T(8,128)(2,1)} %wk_hbm.1, bf16[4096,512]{1,0:T(8,128)(2,1)} %wv_hbm.1, f32[1,256]{1,0:T(1,128)} %bitcast.5, f32[1,256]{1,0:T(1,128)} %bitcast.6, ...), custom_call_target="tpu_custom_call" | custom-call | tf_op jit(solution)/shard_map/frame_attention/pallas_call | solution.py:306
  27.0 0.6 %copy.14 = bf16[8,2048]{1,0:T(8,128)(2,1)} copy(bf16[8,2048]{1,0:T(8,128)(2,1)S(1)} %frame_attention.1) | data formatting | bytes 65536

commit v6 on v5

--- a/solution.py
+++ b/solution.py
@@ -22,8 +22,8 @@
     tok_hbm, frames_hbm, gain_hbm, wk_hbm, wv_hbm, kb_hbm, vb_hbm, q_hbm, ck_hbm, cv_hbm, start_hbm, len_hbm,
     out_ref,
     tok, frames, gain, weights, kb, vb, q, ck, cv, start, length,
-    normed, square_out, square_in, part_out, part_in, own_part, onehot, send, recv, line_tok, all_tok, cached,
-    sem_in, sem_w, sem_sq, sem_part_s, sem_part_r, sem_data_s, sem_data_r, sem_line, sem_all, know1, know2,
+    normed, square_out, square_in, part_out, part_in, own_part, top_out, top_in, onehot, send, recv, line_tok, all_tok, cached,
+    sem_in, sem_w, sem_sq, sem_part_s, sem_part_r, sem_top_s, sem_top_r, sem_data_s, sem_data_r, sem_line, sem_all, know1, know2,
 ):
     g, s, m = lax.axis_index("grp"), lax.axis_index("seq"), lax.axis_index("mp")
     core, y, z = lax.rem(s, NC), lax.rem(s // NC, NY), s // (NC * NY)
@@ -159,12 +159,22 @@
         for at in range(split):
             piece = product[:, at * width : (at + 1) * width]
             j = i * split + at
-            part_out[j] = piece
+            biggest = jnp.maximum(jnp.max(jnp.abs(piece), axis=1, keepdims=True), 1e-30)
+            part_out[j] = jnp.round(piece * (32767.0 / biggest)).astype(jnp.int32).astype(jnp.int16)
+            tall = jnp.concatenate(
+                [jnp.broadcast_to(biggest, (rows, lanes)), jnp.zeros((lanes - rows, lanes), F32)], axis=0
+            )
+            top_out[j] = tall.T[:1]
             copy = pltpu.make_async_remote_copy(
                 part_out.at[j], part_in.at[j], sem_part_s.at[j], sem_part_r.at[j], device_id=other, device_id_type=MESH
             )
             copy.start()
             part_copies.append(copy)
+            copy = pltpu.make_async_remote_copy(
+                top_out.at[j], top_in.at[j], sem_top_s.at[j], sem_top_r.at[j], device_id=other, device_id_type=MESH
+            )
+            copy.start()
+            top_copies.append(copy)
 
     share(first_product, 0)
     for i in range(1, 4):
@@ -217,7 +227,10 @@
     for i in range(2 * split):
         bias = (kb, vb)[i // split][:, (i % split) * width : (i % split + 1) * width]
         part_copies[i].wait()
-        whole = (own_part[i] + part_in[i] + bias).astype(BF16)
+        top_copies[i].wait()
+        top = jnp.broadcast_to(top_in[i], (lanes, lanes)).T[:rows, :1] * (1.0 / 32767.0)
+        theirs = part_in[i].astype(jnp.int32).astype(F32) * top
+        whole = (own_part[i] + theirs + bias).astype(BF16)
         parts = []
         for h in range(width // HEAD):
             parts.append(whole[:, h * HEAD : (h + 1) * HEAD])
@@ -312,11 +325,11 @@
             vm((1, rows), jnp.int32), vm((rows, depth), BF16), vm((1, depth), F32), vm((4, depth, half), BF16),
             vm((1, half), F32), vm((1, half), F32), vm(queries.shape, BF16), vm(cache_key.shape, BF16),
             vm(cache_value.shape, BF16), pltpu.SMEM((8,), jnp.int32), pltpu.SMEM((8,), jnp.int32),
-            vm((rows, depth), BF16), vm((1, 128), F32), vm((1, 128), F32), vm((2, rows, half), F32),
-            vm((2, rows, half), F32), vm((2, rows, half), F32), vm((PARTS * 4, 256), BF16),
+            vm((rows, depth), BF16), vm((1, 128), F32), vm((1, 128), F32), vm((2, rows, half), jnp.int16),
+            vm((2, rows, half), jnp.int16), vm((2, rows, half), F32), vm((2, 1, 128), F32), vm((2, 1, 128), F32), vm((PARTS * 4, 256), BF16),
             vm((2, PARTS, 4, HEAD), BF16), vm((2, PARTS, 4, HEAD), BF16), vm((NZ, 1, 128), F32), vm((16, NZ, 1, 128), F32),
             vm((128, 128), F32),
-            dma((16,)), dma((4,)), dma((2,)), dma((2,)), dma((2,)), dma((2,)), dma((2,)), dma((2,)), dma((2,)),
+            dma((16,)), dma((4,)), dma((2,)), dma((2,)), dma((2,)), dma((2,)), dma((2,)), dma((2,)), dma((2,)), dma((2,)), dma((2,)),
             regular, regular,
         ],
         compiler_params=pltpu.CompilerParams(

time: 27.7 us -> 27.5 us (level)
  no operation moved by 1% of the time
where the time goes in v6:
time: 27.5 us; the launch traced here: 27.4 us
  Pallas kernels  26.8 us (97%)
  local copies, waits for them, and re-layouts  0.62 us (2%)
    pallas_call x1, Pallas kernels, local(): pl.pallas_call(kernel, out_shape=pltpu.VMEM(queries.shape, BF16), in_spec...  26.8 us
    unnamed x1, local copies, waits for them, and re-layouts  0.62 us

profile of v6, /device:TPU:1, one launch (start us, length us, event | category | flops | bytes accessed | tf_op | source)
XLA Modules:
  0.0 27.4 jit_solution(283384460992558532)
XLA Ops:
  0.0 26.8 %frame_attention.1 = bf16[8,2048]{1,0:T(8,128)(2,1)S(1)} custom-call(s32[1,96]{1,0:T(1,128)} %bitcast.7, bf16[96,4096]{1,0:T(8,128)(2,1)} %frames_hbm.1, f32[1,4096]{1,0:T(1,128)} %bitcast.4, bf16[4096,512]{1,0:T(8,128)(2,1)} %wk_hbm.1, bf16[4096,512]{1,0:T(8,128)(2,1)} %wv_hbm.1, f32[1,256]{1,0:T(1,128)} %bitcast.5, f32[1,256]{1,0:T(1,128)} %bitcast.6, ...), custom_call_target="tpu_custom_call" | custom-call | tf_op jit(solution)/shard_map/frame_attention/pallas_call | solution.py:319
  26.8 0.6 %copy.14 = bf16[8,2048]{1,0:T(8,128)(2,1)} copy(bf16[8,2048]{1,0:T(8,128)(2,1)S(1)} %frame_attention.1) | data formatting | bytes 65536

commit v7 on v5

--- a/solution.py
+++ b/solution.py
@@ -51,7 +51,6 @@
     near = [other] + [turned(0, d, 0, 0) for d in (1, 2, NZ - 2, NZ - 1)]
     near += [turned(0, 0, dy, dc) for dy in range(NY) for dc in range(NC) if dy or dc]
     near += [turned(1, 0, 0, dc) for dc in range(NC)]
-    tell(barrier, near)
 
     chunk = 32
     loads = [
@@ -76,6 +75,7 @@
     ]
     for load in loads:
         load.start()
+    tell(barrier, near)
     gain_load.start()
     tok_load.start()
     weight_loads = []
@@ -214,6 +214,7 @@
         for dz in (4, 3, 5, 2, 6, 1, 7, 0) for dg in (1, 0) for dy in (2, 1, 3, 0) for dc in (0, 1)
         if dg or dz or dy or dc
     ]
+    peers.sort(key=lambda t: -(2 * t[0] + min(t[1], NZ - t[1]) + min(t[2], NY - t[2])))
     for i in range(2 * split):
         bias = (kb, vb)[i // split][:, (i % split) * width : (i % split + 1) * width]
         part_copies[i].wait()

time: 27.7 us -> 27.7 us (level)
  no operation moved by 1% of the time
where the time goes in v7:
time: 27.7 us
  Pallas kernels  27 us (97%)
  local copies, waits for them, and re-layouts  0.62 us (2%)
    pallas_call x1, Pallas kernels, local(): pl.pallas_call(kernel, out_shape=pltpu.VMEM(queries.shape, BF16), in_spec...  27 us
    unnamed x1, local copies, waits for them, and re-layouts  0.62 us

profile of v7, /device:TPU:1, one launch (start us, length us, event | category | flops | bytes accessed | tf_op | source)
XLA Modules:
  0.0 27.7 jit_solution(10729196331247615368)
XLA Ops:
  0.0 27.0 %frame_attention.1 = bf16[8,2048]{1,0:T(8,128)(2,1)S(1)} custom-call(s32[1,96]{1,0:T(1,128)} %bitcast.7, bf16[96,4096]{1,0:T(8,128)(2,1)} %frames_hbm.1, f32[1,4096]{1,0:T(1,128)} %bitcast.4, bf16[4096,512]{1,0:T(8,128)(2,1)} %wk_hbm.1, bf16[4096,512]{1,0:T(8,128)(2,1)} %wv_hbm.1, f32[1,256]{1,0:T(1,128)} %bitcast.5, f32[1,256]{1,0:T(1,128)} %bitcast.6, ...), custom_call_target="tpu_custom_call" | custom-call | tf_op jit(solution)/shard_map/frame_attention/pallas_call | solution.py:307
  27.1 0.6 %copy.14 = bf16[8,2048]{1,0:T(8,128)(2,1)} copy(bf16[8,2048]{1,0:T(8,128)(2,1)S(1)} %frame_attention.1) | data formatting | bytes 65536
